TPU v7x, 32 devices: a whole 2x2x4 slice. The times are simulated.
32 devices in a mesh: band: 4 (over z), px: 4 (over x, core), py: 2 (over y).
Axes of the slice: x: 2, y: 2, z: 4, core: 2. Of those that a mesh axis runs over, the one named last changes fastest.
Arguments:
- orbitals: bfloat16 [4, 1024, 384], P('band', ('px', 'py')), may hold values from -0.01171875 to 0.01171875
- occupations: float32 [4], P('band'), may hold values from 0.2 to 2
- stick_map: int32 [2, 1024], P(None, 'px'), may hold values from 0 to 191, as said below
- core_density: float32 [192, 192, 192], P('py', 'px'), may hold values from 0.05 to 0.5
Outputs:
- potential: float32 [192, 192, 192], P('py', 'px')
- gradient: float32 [3, 192, 192, 192], P(None, 'py', 'px')
Inputs may be any that keep to these rules, and one draw needn't show every extreme that they name: `stick_map`: columns i * 128 * 2 to (i + 1) * 128 * 2 - 1 have x index from i * 48 to (i + 1) * 48 - 1; no two columns share a grid position.
All inputs are finite; a program needn't handle non-finite values.
Results may differ from a plain program's by a relative error of at most 0.0054.
Values may be sent and summed in bfloat16 or wider, within the bound.
A program may use at most 128 MiB of HBM per device.

v0:
```python
import math

import jax
import jax.numpy as jnp
from jax import lax
from jax.sharding import PartitionSpec as P

SPACING = 0.25
PBE_KAPPA = 0.804
PBE_MU = 0.2195
SLATER_COEF = 0.75 * (3.0 / math.pi) ** (1.0 / 3.0)
REDUCED_SCALE = 4.0 * (3.0 * math.pi**2) ** (2.0 / 3.0)
HIGHEST_PREC = lax.Precision.HIGHEST


def complex_table(row_index, col_index, points, direction):
    product = row_index[:, None] * col_index[None, :] % points
    angles = 2.0 * math.pi / points * product.astype(jnp.float32)
    cosine = jnp.cos(angles)
    sine_part = direction * jnp.sin(angles)
    return jnp.stack([jnp.stack([cosine, sine_part], 1), jnp.stack([-sine_part, cosine], 1)], 0)


def freq_pair(positions, points):
    signed = jnp.where(positions <= points // 2, positions, positions - points).astype(jnp.float32)
    gradient_freq = jnp.where(positions == points // 2, 0.0, signed)
    return (signed, gradient_freq)


def swap_rows(values):
    return lax.all_to_all(values, "px", split_axis=1, concat_axis=0, tiled=True)


def swap_depth(values):
    moved = lax.all_to_all(values, ("band", "py"), split_axis=1, concat_axis=0, tiled=True)
    return moved


def exchange_part(density, fields):
    cube_root = jnp.cbrt(density)
    four_thirds = density * cube_root
    grad_square = fields[1] * fields[1] + fields[2] * fields[2] + fields[3] * fields[3]
    reduced = grad_square / (REDUCED_SCALE * four_thirds * four_thirds)
    denominator = 1.0 + PBE_MU * reduced / PBE_KAPPA
    enhance = 1.0 + PBE_KAPPA - PBE_KAPPA / denominator
    enhance_slope = PBE_MU / (denominator * denominator)
    potential = fields[0] - SLATER_COEF * cube_root * (
        4.0 / 3.0 * enhance - 8.0 / 3.0 * reduced * enhance_slope
    )
    return jnp.concatenate([potential[None], fields[1:]], 0)


def transform(rho_local, pieces, depth_index, px_index):
    zshare, y_rows, points = rho_local.shape
    rows_px = lax.axis_size("px")
    rows_py = lax.axis_size("py")
    xblock = points // rows_px
    kyblock = points // pieces
    zblock = zshare * (pieces // rows_py)
    every_index = jnp.arange(points, dtype=jnp.int32)
    forward = complex_table(every_index, every_index, points, -1.0)
    x_table = forward[0].reshape(points, 2, rows_px, xblock).transpose(0, 2, 1, 3)
    section_data = jnp.einsum("zyx,xbsk->ybzsk", rho_local, x_table, precision=HIGHEST_PREC)
    section_data = swap_rows(section_data.reshape(y_rows, rows_px, zshare * 2 * xblock))
    section_data = section_data.reshape(points, zshare, 2, xblock)
    y_table = forward.reshape(2, points, 2, pieces, kyblock)
    section_data = jnp.einsum("yzrx,rysdk->zdksx", section_data, y_table, precision=HIGHEST_PREC)
    section_data = swap_depth(section_data.reshape(zshare, pieces, kyblock * 2 * xblock))
    section_data = section_data.reshape(pieces * zshare, kyblock, 2, xblock)
    source = jnp.arange(pieces * zshare, dtype=jnp.int32)
    device = source // zshare
    within = source % zshare
    z_order = device % rows_py * zblock + device // rows_py * zshare + within
    z_table = complex_table(z_order, every_index, points, -1.0)
    spectrum = jnp.einsum("zyrx,rzsk->kysx", section_data, z_table, precision=HIGHEST_PREC)
    q_depth, g_depth = freq_pair(every_index, points)
    ky_index = depth_index * kyblock + jnp.arange(kyblock, dtype=jnp.int32)
    q_col, g_col = freq_pair(ky_index, points)
    kx_index = px_index * xblock + jnp.arange(xblock, dtype=jnp.int32)
    q_row, g_row = freq_pair(kx_index, points)
    wave_unit = 2.0 * math.pi / (points * SPACING)
    squared = wave_unit**2 * (
        q_depth[:, None, None] ** 2 + q_col[None, :, None] ** 2 + q_row[None, None, :] ** 2
    )
    hartree = jnp.where(squared > 0, 4.0 * math.pi / jnp.where(squared > 0, squared, 1.0), 0.0)
    wave_z = wave_unit * g_depth[:, None, None]
    wave_y = wave_unit * g_col[None, :, None]
    wave_x = wave_unit * g_row[None, None, :]
    real_part = spectrum[:, :, 0, :]
    imag_part = spectrum[:, :, 1, :]
    first_factor = hartree - wave_x
    packed = jnp.stack(
        [
            jnp.stack([first_factor * real_part, first_factor * imag_part], 2),
            jnp.stack(
                [-wave_z * real_part - wave_y * imag_part, wave_y * real_part - wave_z * imag_part],
                2,
            ),
        ],
        0,
    )
    inverse = complex_table(every_index, every_index, points, 1.0)
    zi_table = complex_table(every_index, z_order, points, 1.0).reshape(
        2, points, 2, pieces, zshare
    )
    section_data = jnp.einsum("fkyrx,rksdz->ydfzsx", packed, zi_table, precision=HIGHEST_PREC)
    section_data = swap_depth(section_data.reshape(kyblock, pieces, 2 * zshare * 2 * xblock))
    section_data = section_data.reshape(points, 2, zshare, 2, xblock)
    yi_table = inverse.reshape(2, points, 2, rows_px, y_rows)
    section_data = jnp.einsum("kfzrx,rksby->xbfzsy", section_data, yi_table, precision=HIGHEST_PREC)
    section_data = swap_rows(section_data.reshape(xblock, rows_px, 2 * zshare * 2 * y_rows))
    section_data = section_data.reshape(points, 2, zshare, 2, y_rows)
    fields = jnp.einsum("kfzry,rksx->fszyx", section_data, inverse, precision=HIGHEST_PREC)
    fields = fields * (1.0 / float(points) ** 3)
    return fields.reshape(4, zshare, y_rows, points)


def body(orbitals, occupations, stick_map, core_density):
    bands_here, columns_here, doubled = orbitals.shape
    points = doubled // 2
    rows_px = lax.axis_size("px")
    rows_py = lax.axis_size("py")
    groups = lax.axis_size("band")
    px_index = lax.axis_index("px")
    py_index = lax.axis_index("py")
    xblock = points // rows_px
    zblock = points // rows_py
    y_rows = points // rows_px
    every_index = jnp.arange(points, dtype=jnp.int32)
    inverse = complex_table(every_index, every_index, points, 1.0)
    z_table = (
        inverse.reshape(2, points, 2, rows_py, zblock)
        .transpose(0, 1, 3, 2, 4)
        .reshape(doubled, doubled)
    )
    columns = jnp.dot(
        orbitals.astype(jnp.float32).reshape(bands_here * columns_here, doubled),
        z_table,
        precision=HIGHEST_PREC,
    )
    columns = columns.astype(jnp.bfloat16).reshape(bands_here, columns_here, doubled)
    columns = lax.all_to_all(columns, "py", split_axis=2, concat_axis=1, tiled=True)
    slot_index = stick_map[1] * xblock + (stick_map[0] - px_index * xblock)
    plane_data = (
        jnp.zeros((bands_here, points * xblock, 2 * zblock), jnp.float32)
        .at[:, slot_index]
        .set(columns.astype(jnp.float32))
    )
    plane_data = plane_data.reshape(bands_here, points, xblock, 2, zblock)
    plane_data = jnp.einsum("byxrz,rysk->bkxsz", plane_data, inverse, precision=HIGHEST_PREC)
    plane_data = plane_data.astype(jnp.bfloat16).reshape(bands_here, points, xblock * 2 * zblock)
    plane_data = lax.all_to_all(plane_data, "px", split_axis=1, concat_axis=2, tiled=True)
    plane_data = plane_data.astype(jnp.float32).reshape(bands_here, y_rows, points, 2, zblock)
    orbital_values = jnp.einsum("byxrz,rxsk->bszyk", plane_data, inverse, precision=HIGHEST_PREC)
    density = jnp.einsum(
        "b,bszyk->zyk", occupations, orbital_values * orbital_values, precision=HIGHEST_PREC
    )
    zshare = zblock // groups
    band_index = lax.axis_index("band")
    shared_rows = lax.psum_scatter(density, "band", scatter_dimension=0, tiled=True)
    core_rows = lax.dynamic_slice_in_dim(core_density, band_index * zshare, zshare, 0)
    rho_local = shared_rows + core_rows
    fields = transform(rho_local, groups * rows_py, band_index * rows_py + py_index, px_index)
    results = lax.all_gather(exchange_part(rho_local, fields), "band", axis=1, tiled=True)
    return (results[0], results[1:4])


def solution(mesh):
    return jax.shard_map(
        body,
        mesh=mesh,
        in_specs=(P("band", ("px", "py"), None), P("band"), P(None, "px"), P("py", "px", None)),
        out_specs=(P("py", "px", None), P(None, "py", "px", None)),
        check_vma=False,
    )
```

profile of v0, /device:TPU:0, one launch (start us, length us, event | category | flops | bytes accessed | tf_op | source)
XLA Modules:
  0.0 1160.9 jit_solution(13728535052132577211)
XLA Ops:
  27.8 12.3 %reshape.807 = f32[192,48,2,96]{3,2,1,0:T(2,128)} reshape(f32[9216,192]{1,0:T(8,128)} %scatter_custom_fusion) | data formatting | bytes 14155776 | tf_op jit(solution)/shard_map/reshape.2
  40.1 14.2 %copy.140 = f32[192,48,2,96]{0,3,2,1:T(8,128)} copy(f32[192,48,2,96]{3,2,1,0:T(2,128)} %reshape.807) | data formatting | bytes 14155776 | tf_op jit(solution)/shard_map/reshape.2
  54.3 18.6 %fusion.5 = bf16[1,192,48,2,96]{1,4,2,3,0:T(8,128)(2,1)} fusion(f32[192,48,2,96]{0,3,2,1:T(8,128)} %copy.140, f32[1,192,2,192]{3,1,0,2:T(8,128)S(1)} %get-tuple-element.11, f32[1,192,2,192]{3,1,0,2:T(8,128)S(1)} %get-tuple-element.10), kind=kOutput, calls=%fused_computation.8 | convolution fusion | flops 8155643904 | bytes 11206656 | tf_op jit(solution)/shard_map/byxrz,rysk->bkxsz/dot_general | solution.py:150
  72.8 11.6 copy.141
  84.4 24.4 %reshape.857 = bf16[1,192,9216]{2,0,1:T(2,128)(2,1)} reshape(bf16[1,192,48,2,96]{4,3,2,1,0:T(2,128)(2,1)} %copy.141) | data formatting | bytes 7077888 | tf_op jit(solution)/shard_map/reshape | solution.py:151
  108.8 78.5 %reduce.4 = bf16[192,9216]{1,0:T(8,128)(2,1)} reduce(bf16[192,1,9216]{2,1,0:T(2,128)(2,1)} %bitcast.221, bf16[]{:T(256)} %broadcast.1309), dimensions={1}, to_apply=%bitcast.207.reduce_sub_computation | reduce | bytes 7077890
  198.3 40.5 %all-to-all-done.1 = bf16[4,2,221184]{2,1,0:T(2,128)(2,1)} async-done(((bf16[4,2,221184]{2,1,0:T(2,128)(2,1)}), bf16[4,2,221184]{2,1,0:T(2,128)(2,1)}, u32[]{:S(2)}, u32[]{:S(2)}) %all-to-all-start.1) | async-done | bytes 3538976 | tf_op jit(solution)/shard_map/all_to_all | solution.py:152
  254.0 14.9 %reshape.809 = bf16[48,192,2,96]{3,2,1,0:T(2,128)(2,1)} reshape(bf16[1,48,4,9216]{3,2,1,0:T(4,128)(2,1)} %copy.143) | data formatting | bytes 7077888 | tf_op jit(solution)/shard_map/reshape.5
  268.9 10.5 fusion.2
  289.7 84.4 %reduce-scatter.2.cloned.1.call-done = f32[24,48,192]{2,1,0:T(8,128)} async-done(((f32[96,48,192]{2,1,0:T(8,128)}), f32[24,48,192]{2,1,0:T(8,128)}) %reduce-scatter.2.cloned.1.call-update) | async-done | bytes 884752 | tf_op jit(solution)/shard_map/reduce_scatter | solution.py:160
  380.9 7.5 copy.147
  388.4 9.3 reshape.811
  402.4 21.2 %all-to-all-done.2 = f32[48,4,2304]{2,0,1:T(8,128)S(1)} async-done(((f32[48,4,2304]{2,0,1:T(8,128)}), f32[48,4,2304]{2,0,1:T(8,128)S(1)}, u32[]{:S(2)}, u32[]{:S(2)}) %all-to-all-start.2) | async-done | bytes 1769504 | tf_op jit(solution)/shard_map/all_to_all | solution.py:31
  423.6 8.6 reshape.812
  432.2 10.4 fusion.27
  448.4 9.7 reshape.858
  466.9 37.3 %all-to-all-done.3 = f32[24,8,2304]{2,0,1:T(8,128)S(1)} async-done(((f32[24,8,2304]{2,0,1:T(8,128)}), f32[24,8,2304]{2,0,1:T(8,128)S(1)}, u32[]{:S(2)}, u32[]{:S(2)}) %all-to-all-start.3) | async-done | bytes 1769504 | tf_op jit(solution)/shard_map/all_to_all | solution.py:35
  504.1 8.6 reshape.814
  525.6 15.9 %fusion.22 = f32[24,8,2,24,2,48]{5,3,0,2,1,4:T(8,128)S(1)} fusion(f32[1,192,24,2,48]{1,4,2,3,0:T(8,128)S(1)} %maximum_bitcast_fusion.5, f32[1,192,24,2,48]{1,4,2,3,0:T(8,128)S(1)} %maximum_bitcast_fusion.4, f32[1,192,1,8,24]{1,4,0,3,2:T(8,128)S(1)} %copy-done.4, f32[1,192,1,8,24]{1,4,0,3,2:T(8,128)S(1)} %copy-done.3, ...), kind=kOutput, calls=%fused_computation.28 | convolution fusion | flops 4078190592 | bytes 7520256 | tf_op jit(solution)/shard_map/fkyrx,rksdz->ydfzsx/dot_general | solution.py:106
  541.5 8.0 copy.189
  549.5 16.6 %reshape.859 = f32[24,8,4608]{2,0,1:T(8,128)} reshape(f32[24,8,2,24,2,48]{5,4,3,2,0,1:T(2,128)} %copy.189) | data formatting | bytes 7077888 | tf_op jit(solution)/shard_map/reshape | solution.py:107
  571.5 77.6 %all-to-all-done.4 = f32[24,8,4608]{2,0,1:T(8,128)} async-done(((f32[24,8,4608]{2,0,1:T(8,128)}), f32[24,8,4608]{2,0,1:T(8,128)}, u32[]{:S(2)}, u32[]{:S(2)}) %all-to-all-start.4) | async-done | bytes 3538976 | tf_op jit(solution)/shard_map/all_to_all | solution.py:35
  649.2 17.3 %reshape.816 = f32[192,2,24,2,48]{4,3,2,1,0:T(2,128)} reshape(f32[8,24,1,4608]{3,1,0,2:T(8,128)} %bitcast.63) | data formatting | bytes 7077888 | tf_op jit(solution)/shard_map/reshape | solution.py:108
  666.5 24.9 %fusion.19 = f32[48,4,2,24,2,48]{0,5,3,2,1,4:T(8,128)} fusion(f32[192,2,24,2,48,1,1]{4,3,2,1,0,6,5:T(2,128)} %bitcast.218, f32[1,192,1,4,48]{1,4,0,3,2:T(8,128)S(1)} %get-tuple-element.20, f32[1,192,1,4,48]{1,4,0,3,2:T(8,128)S(1)} %get-tuple-element.19, f32[1,192,1,4,48]{1,4,0,3,2:T(8,128)S(1)} %get-tuple-element.18), kind=kOutput, calls=%fused_computation.27 | convolution fusion | flops 4077305856 | bytes 7520256 | tf_op jit(solution)/shard_map/kfzrx,rksby->xbfzsy/dot_general | solution.py:110
  691.4 13.7 %copy.157 = f32[48,4,2,24,2,48]{5,4,3,2,0,1:T(2,128)} copy(f32[48,4,2,24,2,48]{0,5,3,2,1,4:T(8,128)} %fusion.19) | data formatting | bytes 7077888 | tf_op jit(solution)/shard_map/kfzrx,rksby->xbfzsy/transpose | solution.py:110
  705.1 16.6 %reshape.817 = f32[48,4,4608]{2,0,1:T(8,128)} reshape(f32[48,4,2,24,2,48]{5,4,3,2,0,1:T(2,128)} %copy.157) | data formatting | bytes 7077888 | tf_op jit(solution)/shard_map/reshape | solution.py:111
  721.7 46.9 %all_to_all.84 = f32[48,4,4608]{2,0,1:T(8,128)} all-to-all(f32[48,4,4608]{2,0,1:T(8,128)} %reshape.817), channel_id=1, replica_groups=mesh['band'=4,'px'=4,'py'=2] {'px'}, dimensions={1} | all-to-all | bytes 7077888 | tf_op jit(solution)/shard_map/all_to_all | solution.py:31
  768.6 17.1 %reshape.818 = f32[192,2,24,2,48]{4,3,2,1,0:T(2,128)} reshape(f32[4,48,1,4608]{3,1,0,2:T(8,128)} %bitcast.224) | data formatting | bytes 7077888 | tf_op jit(solution)/shard_map/reshape | solution.py:112
  785.7 13.2 %copy.158 = f32[192,2,24,2,48]{0,4,3,2,1:T(8,128)} copy(f32[192,2,24,2,48]{4,3,2,1,0:T(2,128)} %reshape.818) | data formatting | bytes 7077888 | tf_op jit(solution)/shard_map/reshape | solution.py:112
  798.9 10.3 fusion.9
  816.6 320.4 %all-gather.2.cloned.1.call-done = f32[4,96,48,192]{3,2,1,0:T(8,128)} async-done(((f32[4,24,48,192]{3,2,1,0:T(8,128)}), f32[4,96,48,192]{3,2,1,0:T(8,128)}) %all-gather.2.cloned.1.call-update) | async-done | bytes 14155792 | tf_op jit(solution)/shard_map/all_gather | solution.py:164
  1141.8 11.8 %slice.55 = f32[3,96,48,192]{3,2,1,0:T(8,128)} slice(f32[4,96,48,192]{3,2,1,0:T(8,128)} %all-gather.2.cloned.1.call-done), slice={[1:4], [0:96], [0:48], [0:192]} | slice | bytes 21233664 | tf_op jit(solution)/shard_map/slice | solution.py:165
  (74 shorter events, 112.7 us)
Async XLA Ops:
  7.2 2.2 copy-start
  8.1 10.4 copy-start.5
  12.6 8.6 all-to-all-start
  192.9 45.9 %all-to-all-start.1 = ((bf16[4,2,221184]{2,1,0:T(2,128)(2,1)}), bf16[4,2,221184]{2,1,0:T(2,128)(2,1)}, u32[]{:S(2)}, u32[]{:S(2)}) async-start(bf16[4,2,221184]{2,1,0:T(2,128)(2,1)} %reshape.864), calls=%async_computation.1 | async-start | bytes 7077888 | tf_op jit(solution)/shard_map/all_to_all | solution.py:152
  197.6 176.5 %reduce-scatter.2.cloned.1.call-start = ((), (), s32[]{:S(2)}) async-start(), calls=%async_computation.7 | async-start | bytes 5898240 | tf_op jit(solution)/shard_map/reduce_scatter | solution.py:160
  397.7 25.9 %all-to-all-start.2 = ((f32[48,4,2304]{2,0,1:T(8,128)}), f32[48,4,2304]{2,0,1:T(8,128)S(1)}, u32[]{:S(2)}, u32[]{:S(2)}) async-start(f32[48,4,2304]{2,0,1:T(8,128)} %reshape.811), calls=%async_computation.3 | async-start | bytes 3538944 | tf_op jit(solution)/shard_map/all_to_all | solution.py:31
  458.1 46.0 %all-to-all-start.3 = ((f32[24,8,2304]{2,0,1:T(8,128)}), f32[24,8,2304]{2,0,1:T(8,128)S(1)}, u32[]{:S(2)}, u32[]{:S(2)}) async-start(f32[24,8,2304]{2,0,1:T(8,128)} %reshape.858), calls=%async_computation.4 | async-start | bytes 3538944 | tf_op jit(solution)/shard_map/all_to_all | solution.py:35
  524.6 0.9 copy-start.3
  524.6 1.0 copy-start.4
  566.1 83.1 %all-to-all-start.4 = ((f32[24,8,4608]{2,0,1:T(8,128)}), f32[24,8,4608]{2,0,1:T(8,128)}, u32[]{:S(2)}, u32[]{:S(2)}) async-start(f32[24,8,4608]{2,0,1:T(8,128)} %reshape.859), calls=%async_computation.5 | async-start | bytes 7077888 | tf_op jit(solution)/shard_map/all_to_all | solution.py:35
  570.6 566.4 %all-gather.2.cloned.1.call-start = ((), (), s32[]{:S(2)}) async-start(), calls=%async_computation.8 | async-start | bytes 23592960 | tf_op jit(solution)/shard_map/all_gather | solution.py:164
  809.6 1.3 copy-start.2
  1141.8 11.8 %copy-start.1 = (bf16[1,128,384]{2,1,0:T(8,128)(2,1)S(1)}, bf16[1,128,384]{2,1,0:T(8,128)(2,1)}, u32[]{:S(2)}) copy-start(bf16[1,128,384]{2,1,0:T(8,128)(2,1)} %param.4) | copy-start | bytes 294916
Sparse Core Ops, SparseCore 0:
  288.9 85.1 reduce-scatter.1
  816.7 320.2 all-gather.1
where the time goes:
time: 1170 us; the launch traced here: 1160 us
  waiting for transfers between devices  584 us (50%)
  local copies, waits for them, and re-layouts  291 us (25%)
  matrix products  103 us (9%)
  other arithmetic  98.1 us (8%)
  blocking collectives  46.9 us (4%)
  starting transfers between devices  22.4 us (2%)
  between operations  15.5 us (1%)
    all_gather x1, waiting for transfers between devices, body(): lax.all_gather(exchange_part(rho_local, fields), 'band', axis=1, tiled=True)  320 us
    all_to_all x2, waiting for transfers between devices, swap_depth(): lax.all_to_all(values, ('band', 'py'), split_axis=1, concat_axis=0, tiled...  115 us
    reduce_scatter x1, waiting for transfers between devices, body(): lax.psum_scatter(density, 'band', scatter_dimension=0, tiled=True)  84.4 us
    unnamed x2, other arithmetic  79.7 us
    all_to_all x1, blocking collectives, swap_rows(): return lax.all_to_all(values, 'px', split_axis=1, concat_axis=0, tiled=True)  46.9 us
    another operation x3, local copies, waits for them, and re-layouts  41.4 us
    all_to_all x1, waiting for transfers between devices, body(): lax.all_to_all(plane_data, 'px', split_axis=1, concat_axis=2, tiled=True)  40.5 us
    reshape x2, local copies, waits for them, and re-layouts, transform(): section_data = section_data.reshape(points, 2, zshare, 2, y_rows)  30.3 us
  transfers between devices with their start and end apart: 7, of which 7 were waited for; matrix products, arithmetic and copies ran while one was open for 1% of the time, Pallas kernels for 0%

commit v1 on v0

v1 whole, which is shorter than its diff:
```python
import math

import jax
import jax.numpy as jnp
import numpy as np
from jax import lax
from jax.experimental.layout import Layout, with_layout_constraint
from jax.sharding import PartitionSpec as P

SPACING = 0.25
PBE_KAPPA = 0.804
PBE_MU = 0.2195
SLATER_COEF = 0.75 * (3.0 / math.pi) ** (1.0 / 3.0)
REDUCED_SCALE = 4.0 * (3.0 * math.pi**2) ** (2.0 / 3.0)
BF = jnp.bfloat16
F32 = jnp.float32
HIGH = lax.Precision.HIGH


def inverse_table(points):
    k = np.arange(points)
    angles = 2.0 * np.pi / points * (k[:, None] * k[None, :] % points)
    cosine, sine = np.cos(angles), np.sin(angles)
    return np.stack([np.stack([cosine, sine], 1), np.stack([-sine, cosine], 1)], 0)


def two_halves(table):
    high = table.astype(np.float32).astype(BF)
    low = (table - high.astype(np.float64)).astype(np.float32).astype(BF)
    return high, low


def dot2(spec, data, table):
    high, low = table
    first = jnp.einsum(spec, data, high, preferred_element_type=F32)
    return first + jnp.einsum(spec, data, low, preferred_element_type=F32)


def real_basis(points):
    pos = np.arange(points)
    freq = np.concatenate([np.arange(points // 2 + 1), np.arange(1, points // 2)])
    angle = 2.0 * np.pi / points * (pos[:, None] * freq[None, :] % points)
    basis = np.where(np.arange(points)[None, :] <= points // 2, np.cos(angle), np.sin(angle))
    scale = np.where((freq == 0) | (freq == points // 2), 1.0 / points, 2.0 / points)
    return basis * np.sqrt(scale), freq


def derivative_matrix(points):
    pos = np.arange(points)
    freq = np.arange(1, points // 2)
    unit = 2.0 * np.pi / (points * SPACING)
    lag = (pos[None, :] - pos[:, None]) % points
    values = np.zeros(points)
    for d in range(points):
        values[d] = np.sum(-2.0 * unit * freq * np.sin(2.0 * np.pi * (freq * d % points) / points)) / points
    return values[lag]


def exchange_part(density, hartree, grad_x, grad_y, grad_z):
    cube_root = jnp.cbrt(density)
    four_thirds = density * cube_root
    grad_square = grad_x * grad_x + grad_y * grad_y + grad_z * grad_z
    reduced = grad_square / (REDUCED_SCALE * four_thirds * four_thirds)
    denominator = 1.0 + PBE_MU * reduced / PBE_KAPPA
    enhance = 1.0 + PBE_KAPPA - PBE_KAPPA / denominator
    enhance_slope = PBE_MU / (denominator * denominator)
    return hartree - SLATER_COEF * cube_root * (
        4.0 / 3.0 * enhance - 8.0 / 3.0 * reduced * enhance_slope
    )


def partial_density(orbitals, occupations, stick_map, px_index):
    bands_here, columns_here, doubled = orbitals.shape
    points = doubled // 2
    rows_px = lax.axis_size("px")
    rows_py = lax.axis_size("py")
    xblock = points // rows_px
    zblock = points // rows_py
    inverse = inverse_table(points)
    z_table = two_halves(
        inverse.reshape(2, points, 2, rows_py, zblock).transpose(0, 1, 3, 2, 4).reshape(doubled, doubled)
    )
    columns = dot2("bsk,kw->bsw", orbitals, z_table).astype(BF)
    columns = lax.all_to_all(columns, "py", split_axis=2, concat_axis=1, tiled=True)
    sticks = columns.shape[1]
    columns = columns.reshape(bands_here, sticks, 2, zblock)
    y_hot = (stick_map[1][:, None] == jnp.arange(points, dtype=jnp.int32)[None, :]).astype(BF)
    x_local = stick_map[0] - px_index * xblock
    x_hot = x_local[:, None] == jnp.arange(xblock, dtype=jnp.int32)[None, :]
    by_y = inverse.reshape(2, points, 2, rows_px, xblock).transpose(1, 0, 3, 4, 2)
    picked = [
        jnp.einsum("sy,yipwo->sipwo", y_hot, half, preferred_element_type=F32).astype(BF)
        for half in two_halves(by_y)
    ]
    x_table = two_halves(inverse.reshape(2, rows_px, xblock, 2, points).transpose(1, 0, 2, 3, 4))
    total = None
    for band in range(bands_here):
        spread = jnp.where(x_hot[:, None, :, None], columns[band][:, :, None, :], jnp.zeros((), BF))
        plane = jnp.einsum("sipwo,sixz->pwoxz", picked[0], spread, preferred_element_type=F32)
        plane = plane + jnp.einsum("sipwo,sixz->pwoxz", picked[1], spread, preferred_element_type=F32)
        plane = plane.astype(BF)
        plane = lax.all_to_all(plane, "px", split_axis=0, concat_axis=0, tiled=True)
        values = dot2("pwoxz,poxtk->wztk", plane, x_table)
        weighted = occupations[band] * (values[:, :, 0] * values[:, :, 0] + values[:, :, 1] * values[:, :, 1])
        total = weighted if total is None else total + weighted
    return total


def gathered(field):
    field = with_layout_constraint(field.astype(BF), Layout((0, 1, 2)))
    return lax.all_gather(field, "band", axis=0, tiled=True)


def body(orbitals, occupations, stick_map, core_density):
    points = orbitals.shape[2] // 2
    rows_px = lax.axis_size("px")
    rows_py = lax.axis_size("py")
    groups = lax.axis_size("band")
    px_index = lax.axis_index("px")
    py_index = lax.axis_index("py")
    band_index = lax.axis_index("band")
    yblock = points // rows_px
    xblock = points // rows_px
    zblock = points // rows_py
    zshare = zblock // groups
    pieces = groups * rows_py
    kyblock = points // pieces

    density = partial_density(orbitals, occupations, stick_map, px_index)
    shares = density.astype(BF).reshape(yblock, groups, zshare, points).transpose(1, 0, 2, 3)
    shares = lax.all_to_all(shares, "band", split_axis=0, concat_axis=0, tiled=True)
    core = lax.dynamic_slice_in_dim(core_density, band_index * zshare, zshare, 0)
    rho = shares.astype(F32).sum(0) + core.transpose(1, 0, 2)

    basis, freq = real_basis(points)
    derive = derivative_matrix(points).astype(np.float32)
    basis32 = basis.astype(np.float32)
    data = jnp.einsum("yzx,xpk->pyzk", rho, basis32.reshape(points, rows_px, xblock), precision=HIGH)
    data = lax.all_to_all(data, "px", split_axis=0, concat_axis=0, tiled=True)
    data = data.reshape(points, zshare, xblock)
    high_basis, low_basis = two_halves(basis)
    x_basis = (high_basis.reshape(points, rows_px, xblock), low_basis.reshape(points, rows_px, xblock))
    grad_x = jnp.einsum("yzx,xw->zyw", rho, derive, precision=HIGH)
    every_x = gathered(grad_x)
    lines_y = jnp.einsum("yzk,yw->wzk", data, derive, precision=HIGH).astype(BF)
    lines_y = lines_y.reshape(rows_px, yblock, zshare, xblock)
    lines_y = lax.all_to_all(lines_y, "px", split_axis=0, concat_axis=0, tiled=True)
    grad_y = dot2("pyzk,xpk->zyx", lines_y, x_basis)
    grad_y_sent = grad_y.astype(BF)
    modes = jnp.einsum("yzk,yj->jzk", data, basis32, precision=HIGH)
    modes = modes.reshape(pieces, kyblock, zshare, xblock)
    modes = lax.all_to_all(modes, ("band", "py"), split_axis=0, concat_axis=0, tiled=True)
    source = np.arange(points)
    device, within = source // zshare, source % zshare
    z_order = device % rows_py * zblock + device // rows_py * zshare + within
    z_basis = basis32[z_order].reshape(pieces, zshare, points)
    z_derive = derive[z_order][:, z_order].reshape(pieces, zshare, pieces, zshare)
    spectrum = jnp.einsum("djzk,dzm->mjk", modes, z_basis, precision=HIGH)
    unit = 2.0 * math.pi / (points * SPACING)
    all_q = jnp.asarray((freq * freq).astype(np.float32))
    q_col = lax.dynamic_slice_in_dim(all_q, (band_index * rows_py + py_index) * kyblock, kyblock)
    q_row = lax.dynamic_slice_in_dim(all_q, px_index * xblock, xblock)
    squared = unit**2 * (all_q[:, None, None] + q_col[None, :, None] + q_row[None, None, :])
    factor = jnp.where(squared > 0, 4.0 * math.pi / jnp.where(squared > 0, squared, 1.0), 0.0)
    spectrum = spectrum * factor
    back = jnp.stack(
        [
            jnp.einsum("mjk,dzm->djzk", spectrum, z_basis, precision=HIGH).astype(BF),
            jnp.einsum("ejwk,ewdz->djzk", modes, z_derive, precision=HIGH).astype(BF),
        ],
        1,
    )
    back, every_y = lax.optimization_barrier((back, grad_y_sent))
    every_y = gathered(every_y)
    back = lax.all_to_all(back, ("band", "py"), split_axis=0, concat_axis=0, tiled=True)
    y_basis = (high_basis.reshape(points, pieces, kyblock), low_basis.reshape(points, pieces, kyblock))
    lines = dot2("dfjzk,ydj->fyzk", back, y_basis)
    lines = lines.astype(BF).reshape(2, rows_px, yblock, zshare, xblock)
    lines = lax.all_to_all(lines, "px", split_axis=1, concat_axis=1, tiled=True)
    fields = dot2("fpyzk,xpk->fzyx", lines, x_basis)
    every_z = gathered(fields[1])
    potential = exchange_part(rho.transpose(1, 0, 2), fields[0], grad_x, grad_y, fields[1])
    every_potential = gathered(potential)
    gradient = jnp.stack([every_x.astype(F32), every_y.astype(F32), every_z.astype(F32)])
    return (every_potential.astype(F32), gradient)


def solution(mesh):
    return jax.shard_map(
        body,
        mesh=mesh,
        in_specs=(P("band", ("px", "py"), None), P("band"), P(None, "px"), P("py", "px", None)),
        out_specs=(P("py", "px", None), P(None, "py", "px", None)),
        check_vma=False,
    )
```

time: 1170 us -> 508 us (0.43)
  waiting for transfers between devices: 584 us -> 303 us
  local copies, waits for them, and re-layouts: 291 us -> 50.4 us
  other arithmetic: 98.1 us -> 28.8 us
  matrix products: 103 us -> 45.6 us
  blocking collectives: 46.9 us -> 30.6 us
    all_gather x1 -> x4, waiting for transfers between devices: 320 us -> 137 us  [gathered(): return lax.all_gather(field, 'band', axis=0, tiled=True)]
    reshape x15 -> x4, local copies, waits for them, and re-layouts: 162 us -> 10.9 us  [the longest x2 7.46 us: body(): lines = lines.astype(BF).reshape(2, rows_px, yblock, zshare, xblock)]
    reduce_scatter x1 -> x0, waiting for transfers between devices: 84.4 us -> none  [body(): lax.psum_scatter(density, 'band', scatter_dimension=0, tiled=True)]
    unnamed x2 -> x1, other arithmetic: 79.7 us -> 1.21 us
    dot_general x9 -> x18, matrix products: 103 us -> 43.9 us  [the longest x5 9.85 us: dot2(): first = jnp.einsum(spec, data, high, preferred_element_type=F32)]
    another operation x3 -> x0, local copies, waits for them, and re-layouts: 41.4 us -> none
    transpose x3 -> x1, local copies, waits for them, and re-layouts: 21.8 us -> 0.15 us  [body(): jnp.einsum('yzx,xpk->pyzk', rho, basis32.reshape(points, rows_px, xblock)...]
    all_to_all x1 -> x2, blocking collectives: 46.9 us -> 30.6 us  [the longest x1 15.5 us: body(): lines = lax.all_to_all(lines, 'px', split_axis=1, concat_axis=1, tiled=True)]
  transfers between devices with their start and end apart: 7 -> 10, of which waited for: 7 -> 9; matrix products, arithmetic and copies ran while one was open for 1% -> 10% of each run, Pallas kernels for 0% -> 0%
where the time goes in v1:
time: 508 us; the launch traced here: 501 us
  waiting for transfers between devices  303 us (60%)
  local copies, waits for them, and re-layouts  50.4 us (10%)
  matrix products  45.6 us (9%)
  blocking collectives  30.6 us (6%)
  other arithmetic  28.8 us (6%)
  starting transfers between devices  26.5 us (5%)
  between operations  15.4 us (3%)
    all_gather x4, waiting for transfers between devices, gathered(): return lax.all_gather(field, 'band', axis=0, tiled=True)  137 us
    all_to_all x1, waiting for transfers between devices, body(): lax.all_to_all(shares, 'band', split_axis=0, concat_axis=0, tiled=True)  53.5 us
    all_to_all x1, waiting for transfers between devices, partial_density(): plane = lax.all_to_all(plane, 'px', split_axis=0, concat_axis=0, tiled=True)  53.2 us
    all_to_all x1, waiting for transfers between devices, body(): lax.all_to_all(back, ('band', 'py'), split_axis=0, concat_axis=0, tiled=T...  36.4 us
    unnamed x64, local copies, waits for them, and re-layouts  31.8 us
    all_to_all x1, waiting for transfers between devices, body(): lax.all_to_all(modes, ('band', 'py'), split_axis=0, concat_axis=0, tiled=...  17.7 us
    all_to_all x1, blocking collectives, body(): lines = lax.all_to_all(lines, 'px', split_axis=1, concat_axis=1, tiled=True)  15.5 us
    all_to_all x1, blocking collectives, body(): data = lax.all_to_all(data, 'px', split_axis=0, concat_axis=0, tiled=True)  15.1 us
  transfers between devices with their start and end apart: 10, of which 9 were waited for; matrix products, arithmetic and copies ran while one was open for 10% of the time, Pallas kernels for 0%

profile of v1, /device:TPU:0, one launch (start us, length us, event | category | flops | bytes accessed | tf_op | source)
XLA Modules:
  0.0 500.5 jit_solution(15879912946561793897)
XLA Ops:
  13.1 4.3 all-to-all-start
  18.1 3.6 all-to-all-done
  22.0 5.4 %fusion.4 = f32[4,48,2,48,96,1]{4,1,5,3,2,0:T(8,128)} fusion(pred[256,48]{0,1:T(8,128)(4,1)S(1)} %iota_compare_fusion.1, bf16[256,2,96]{0,2,1:T(8,128)(2,1)S(1)} %broadcast_in_dim.35, bf16[192,2,4,48,2]{0,3,1,4,2:T(8,128)(2,1)S(1)} %copy-done.24, s32[256]{0:T(256)S(1)} %bitcast.247), kind=kOutput, calls=%fused_computation.9 | convolution fusion | flops 1890041856 | bytes 7484416 | tf_op jit(solution)/shard_map/sipwo,sixz->pwoxz/dot_general | solution.py:100
  27.4 6.9 %fusion = bf16[4,48,2,48,96]{4,1,3,2,0:T(8,128)(2,1)} fusion(f32[4,48,2,48,96,1]{4,1,5,3,2,0:T(8,128)} %fusion.4, pred[256,48]{0,1:T(8,128)(4,1)S(1)} %iota_compare_fusion.1, bf16[256,2,96]{0,2,1:T(8,128)(2,1)S(1)} %broadcast_in_dim.35, bf16[192,2,4,48,2]{0,3,1,4,2:T(8,128)(2,1)S(1)} %copy-done.23, s32[256]{0:T(256)S(1)} %bitcast.248), kind=kOutput, calls=%fused_computation.2 | convolution fusion | flops 1893580800 | bytes 11023360 | tf_op jit(solution)/shard_map/sipwo,sixz->pwoxz/dot_general | solution.py:99
  34.3 5.1 %all-to-all-start.1 = ((bf16[4,48,2,48,96]{4,1,3,2,0:T(8,128)(2,1)}), bf16[4,48,2,48,96]{4,1,3,2,0:T(8,128)(2,1)}, u32[]{:S(2)}, u32[]{:S(2)}) async-start(bf16[4,48,2,48,96]{4,1,3,2,0:T(8,128)(2,1)} %fusion), calls=%async_computation.1 | async-start | bytes 9437184 | tf_op jit(solution)/shard_map/all_to_all | solution.py:102
  40.1 53.2 %all-to-all-done.1 = bf16[4,48,2,48,96]{4,1,3,2,0:T(8,128)(2,1)} async-done(((bf16[4,48,2,48,96]{4,1,3,2,0:T(8,128)(2,1)}), bf16[4,48,2,48,96]{4,1,3,2,0:T(8,128)(2,1)}, u32[]{:S(2)}, u32[]{:S(2)}) %all-to-all-start.1) | async-done | bytes 3538976 | tf_op jit(solution)/shard_map/all_to_all | solution.py:102
  93.2 5.6 %fusion.12 = f32[48,96,2,192,1,1]{3,1,5,4,2,0:T(8,128)S(1)} fusion(bf16[4,2,48,2,192,1]{4,2,0,1,3,5:T(8,128)(2,1)S(1)} %copy-done.8, bf16[4,48,2,48,96,1]{4,1,3,2,0,5:T(8,128)(2,1)} %bitcast.21), kind=kOutput, calls=%fused_computation.18 | convolution fusion | flops 1358954496 | bytes 10911744 | tf_op jit(solution)/shard_map/pwoxz,poxtk->wztk/dot_general | solution.py:36
  98.9 5.6 %bitcast_add_fusion = f32[48,96,2,192]{3,1,2,0:T(8,128)S(1)} fusion(f32[48,96,2,192,1,1]{3,1,5,4,2,0:T(8,128)S(1)} %fusion.12, bf16[4,2,48,2,192,1]{4,2,0,1,3,5:T(8,128)(2,1)S(1)} %copy-done.7, bf16[4,48,2,48,96,1]{4,1,3,2,0,5:T(8,128)(2,1)} %bitcast.21), kind=kOutput, calls=%fused_computation | convolution fusion | flops 1360723968 | bytes 17989632 | tf_op jit(solution)/shard_map/pwoxz,poxtk->wztk/dot_general | solution.py:35
  107.2 5.9 %all-to-all-start.2 = ((bf16[4,48,24,192]{3,2,1,0:T(8,128)(2,1)}), bf16[4,48,24,192]{3,2,1,0:T(8,128)(2,1)S(1)}, u32[]{:S(2)}, u32[]{:S(2)}) async-start(bf16[4,48,24,192]{3,2,1,0:T(8,128)(2,1)} %bitcast.232), calls=%async_computation.2 | async-start | bytes 4718592 | tf_op jit(solution)/shard_map/all_to_all | solution.py:131
  113.1 53.5 %all-to-all-done.2 = bf16[4,48,24,192]{3,2,1,0:T(8,128)(2,1)S(1)} async-done(((bf16[4,48,24,192]{3,2,1,0:T(8,128)(2,1)}), bf16[4,48,24,192]{3,2,1,0:T(8,128)(2,1)S(1)}, u32[]{:S(2)}, u32[]{:S(2)}) %all-to-all-start.2) | async-done | bytes 1769504 | tf_op jit(solution)/shard_map/all_to_all | solution.py:131
  173.3 15.1 %all_to_all.50 = f32[4,1,55296]{2,1,0:T(1,128)S(1)} all-to-all(f32[4,1,55296]{2,1,0:T(1,128)S(1)} %reshape.140), channel_id=1, replica_groups=mesh['band'=4,'px'=4,'py'=2] {'px'}, dimensions={0} | all-to-all | bytes 1769472 | tf_op jit(solution)/shard_map/all_to_all | solution.py:139
  188.9 3.2 reduce.1
  192.1 2.5 reshape.141
  198.8 2.7 reshape.144
  201.4 3.6 all-to-all-start.5
  209.0 3.2 reshape.142
  213.0 3.6 all-to-all-start.4
  221.3 17.7 %all-to-all-done.4 = f32[8,1,27648]{2,1,0:T(1,128)S(1)} async-done(((f32[8,1,27648]{2,1,0:T(1,128)}), f32[8,1,27648]{2,1,0:T(1,128)S(1)}, u32[]{:S(2)}, u32[]{:S(2)}) %all-to-all-start.4) | async-done | bytes 884768 | tf_op jit(solution)/shard_map/all_to_all | solution.py:152
  239.0 2.7 reduce.2
  248.7 4.9 reshape.146
  253.6 3.6 all-to-all-start.6
  258.0 36.4 %all-to-all-done.6 = bf16[8,2,27648]{2,1,0:T(2,128)(2,1)S(1)} async-done(((bf16[8,2,27648]{2,1,0:T(2,128)(2,1)}), bf16[8,2,27648]{2,1,0:T(2,128)(2,1)S(1)}, u32[]{:S(2)}, u32[]{:S(2)}) %all-to-all-start.6) | async-done | bytes 884768 | tf_op jit(solution)/shard_map/all_to_all | solution.py:175
  299.5 4.0 reshape.102
  303.5 3.5 copy.111
  307.0 4.8 reshape.148
  311.8 15.5 %all_to_all.51 = bf16[4,2,55296]{2,1,0:T(2,128)(2,1)S(1)} all-to-all(bf16[4,2,55296]{2,1,0:T(2,128)(2,1)S(1)} %reshape.148), channel_id=1, replica_groups=mesh['band'=4,'px'=4,'py'=2] {'px'}, dimensions={0} | all-to-all | bytes 1769472 | tf_op jit(solution)/shard_map/all_to_all | solution.py:179
  332.2 6.2 %fusion.58 = (bf16[24,48,192]{2,1,0:T(8,128)(2,1)}, bf16[48,24,192]{2,0,1:T(8,128)(2,1)}) fusion(f32[2,24,48,192]{3,2,1,0:T(8,128)S(1)} %fusion.20, f32[48,24,192]{2,0,1:T(8,128)S(1)} %copy-done.3, f32[48,24,192]{2,1,0:T(8,128)S(1)} %copy-done.5, f32[96,48,192]{2,1,0:T(8,128)} %param.27, s32[]{:T(128)S(6)} %select_n.21, f32[192,192,1]{1,0,2:T(8,128)S(1)} %copy-done.13), kind=kOutput, calls=%fused_computation.68 | convolution fusion | flops 260554752 | bytes 9339904 | tf_op jit(solution)/shard_map/yzx,xw->zyw/dot_general | solution.py:143
  341.3 47.2 %all-gather.7.cloned.1.call-done = bf16[96,48,192]{2,1,0:T(8,128)(2,1)} async-done(((bf16[24,48,192]{2,1,0:T(8,128)(2,1)}), bf16[96,48,192]{2,1,0:T(8,128)(2,1)}) %all-gather.7.cloned.1.call-update) | async-done | bytes 1769488 | tf_op jit(solution)/shard_map/all_gather | solution.py:111
  388.5 50.4 %all-gather.11.cloned.1.call-done = bf16[96,48,192]{2,1,0:T(8,128)(2,1)} async-done(((bf16[24,48,192]{2,1,0:T(8,128)(2,1)}), bf16[96,48,192]{2,1,0:T(8,128)(2,1)}) %all-gather.11.cloned.1.call-update) | async-done | bytes 1769488 | tf_op jit(solution)/shard_map/all_gather | solution.py:111
  438.9 10.5 %maximum_convert_fusion = f32[3,96,48,192]{3,2,1,0:T(8,128)} fusion(bf16[1,96,48,192]{3,2,1,0:T(8,128)(2,1)} %bitcast.241, bf16[1,96,48,192]{3,2,1,0:T(8,128)(2,1)} %bitcast.239, bf16[1,96,48,192]{3,2,1,0:T(8,128)(2,1)} %bitcast.240), kind=kLoop, calls=%fused_computation.3 | loop fusion | flops 7962624 | bytes 15925248 | tf_op jit(solution)/shard_map/stack | solution.py:184
  449.4 39.7 %all-gather.5.cloned.1.call-done = bf16[96,48,192]{2,1,0:T(8,128)(2,1)} async-done(((bf16[24,48,192]{2,1,0:T(8,128)(2,1)}), bf16[96,48,192]{2,1,0:T(8,128)(2,1)}) %all-gather.5.cloned.1.call-update) | async-done | bytes 1769488 | tf_op jit(solution)/shard_map/all_gather | solution.py:111
  489.1 4.5 convert_element_type.96
  (105 shorter events, 50.7 us)
Async XLA Ops:
  7.2 14.8 %copy-start.24 = (bf16[192,2,4,48,2]{0,3,1,4,2:T(8,128)(2,1)S(1)}, bf16[192,2,4,48,2]{0,3,1,4,2:T(8,128)(2,1)}, u32[]{:S(2)}) copy-start(bf16[192,2,4,48,2]{0,3,1,4,2:T(8,128)(2,1)} %constant.87.clone) | copy-start | bytes 884740
  13.1 8.6 %all-to-all-start = ((bf16[2,2,12288]{2,1,0:T(2,128)(2,1)}), bf16[2,2,12288]{2,1,0:T(2,128)(2,1)S(1)}, u32[]{:S(2)}, u32[]{:S(2)}) async-start(bf16[2,2,12288]{2,1,0:T(2,128)(2,1)} %reshape.138), calls=%async_computation | async-start | bytes 196608 | tf_op jit(solution)/shard_map/all_to_all | solution.py:84
  22.0 5.4 %copy-start.23 = (bf16[192,2,4,48,2]{0,3,1,4,2:T(8,128)(2,1)S(1)}, bf16[192,2,4,48,2]{0,3,1,4,2:T(8,128)(2,1)}, u32[]{:S(2)}) copy-start(bf16[192,2,4,48,2]{0,3,1,4,2:T(8,128)(2,1)} %constant.86.clone) | copy-start | bytes 884740
  34.3 58.9 %copy-start.8 = (bf16[4,2,48,2,192,1]{4,2,0,1,3,5:T(8,128)(2,1)S(1)}, bf16[4,2,48,2,192,1]{4,2,0,1,3,5:T(8,128)(2,1)}, u32[]{:S(2)}) copy-start(bf16[4,2,48,2,192,1]{4,2,0,1,3,5:T(8,128)(2,1)} %constant.104) | copy-start | bytes 884740
  34.3 58.9 %all-to-all-start.1 = ((bf16[4,48,2,48,96]{4,1,3,2,0:T(8,128)(2,1)}), bf16[4,48,2,48,96]{4,1,3,2,0:T(8,128)(2,1)}, u32[]{:S(2)}, u32[]{:S(2)}) async-start(bf16[4,48,2,48,96]{4,1,3,2,0:T(8,128)(2,1)} %fusion), calls=%async_computation.1 | async-start | bytes 9437184 | tf_op jit(solution)/shard_map/all_to_all | solution.py:102
  93.2 5.6 %copy-start.7 = (bf16[4,2,48,2,192,1]{4,2,0,1,3,5:T(8,128)(2,1)S(1)}, bf16[4,2,48,2,192,1]{4,2,0,1,3,5:T(8,128)(2,1)}, u32[]{:S(2)}) copy-start(bf16[4,2,48,2,192,1]{4,2,0,1,3,5:T(8,128)(2,1)} %constant.103) | copy-start | bytes 884740
  107.2 59.4 %all-to-all-start.2 = ((bf16[4,48,24,192]{3,2,1,0:T(8,128)(2,1)}), bf16[4,48,24,192]{3,2,1,0:T(8,128)(2,1)S(1)}, u32[]{:S(2)}, u32[]{:S(2)}) async-start(bf16[4,48,24,192]{3,2,1,0:T(8,128)(2,1)} %bitcast.232), calls=%async_computation.2 | async-start | bytes 4718592 | tf_op jit(solution)/shard_map/all_to_all | solution.py:131
  167.0 3.8 copy-start.4
  167.0 2.2 copy-start.9
  194.6 2.4 copy-start.12
  197.6 7.5 %copy-start.11 = (f32[192,192]{1,0:T(8,128)S(1)}, f32[192,192]{1,0:T(8,128)}, u32[]{:S(2)}) copy-start(f32[192,192]{1,0:T(8,128)} %constant.94.clone) | copy-start | bytes 442372
  201.4 11.5 %all-to-all-start.5 = ((bf16[4,2,27648]{2,1,0:T(2,128)(2,1)}), bf16[4,2,27648]{2,1,0:T(2,128)(2,1)S(1)}, u32[]{:S(2)}, u32[]{:S(2)}) async-start(bf16[4,2,27648]{2,1,0:T(2,128)(2,1)} %reshape.144), calls=%async_computation.5 | async-start | bytes 884736 | tf_op jit(solution)/shard_map/all_to_all | solution.py:147
  209.0 7.6 %copy-start.21 = (f32[192]{0:T(256)S(1)}, f32[192]{0:T(256)}, u32[]{:S(2)}) copy-start(f32[192]{0:T(256)} %constant.96.clone) | copy-start | bytes 2308
  212.2 6.3 %copy-start.15 = (bf16[192,4,48,1]{0,2,1,3:T(8,128)(2,1)S(1)}, bf16[192,4,48,1]{0,2,1,3:T(8,128)(2,1)}, u32[]{:S(2)}) copy-start(bf16[192,4,48,1]{0,2,1,3:T(8,128)(2,1)} %constant.109) | copy-start | bytes 221188
  213.0 26.0 %all-to-all-start.4 = ((f32[8,1,27648]{2,1,0:T(1,128)}), f32[8,1,27648]{2,1,0:T(1,128)S(1)}, u32[]{:S(2)}, u32[]{:S(2)}) async-start(f32[8,1,27648]{2,1,0:T(1,128)} %reshape.142), calls=%async_computation.4 | async-start | bytes 1769472 | tf_op jit(solution)/shard_map/all_to_all | solution.py:152
  216.5 2.5 copy-start.19
  219.4 1.0 copy-start.2
  221.3 21.4 %copy-start.10 = (f32[8,24,192,1]{2,1,0,3:T(8,128)S(1)}, f32[8,24,192,1]{2,1,0,3:T(8,128)}, u32[]{:S(2)}) copy-start(f32[8,24,192,1]{2,1,0,3:T(8,128)} %constant.102) | copy-start | bytes 442372
  221.3 21.4 %copy-start.20 = (f32[192,24]{0,1:T(8,128)S(1)}, f32[192,24]{0,1:T(8,128)}, u32[]{:S(2)}) copy-start(f32[192,24]{0,1:T(8,128)} %broadcast_add_fusion) | copy-start | bytes 55300
  245.1 1.1 copy-start.22
  253.6 40.8 %all-to-all-start.6 = ((bf16[8,2,27648]{2,1,0:T(2,128)(2,1)}), bf16[8,2,27648]{2,1,0:T(2,128)(2,1)S(1)}, u32[]{:S(2)}, u32[]{:S(2)}) async-start(bf16[8,2,27648]{2,1,0:T(2,128)(2,1)} %reshape.146), calls=%async_computation.6 | async-start | bytes 1769472 | tf_op jit(solution)/shard_map/all_to_all | solution.py:175
  257.2 39.5 %copy-start.18 = (bf16[192,8,24,1,1]{0,2,1,4,3:T(8,128)(2,1)S(1)}, bf16[192,8,24,1,1]{0,2,1,4,3:T(8,128)(2,1)}, u32[]{:S(2)}) copy-start(bf16[192,8,24,1,1]{0,2,1,4,3:T(8,128)(2,1)} %constant.111) | copy-start | bytes 221188
  257.3 84.0 %all-gather.9.cloned.1.call-start = ((), (), s32[]{:S(2)}) async-start(), calls=%async_computation.10 | async-start | bytes 2949120 | tf_op jit(solution)/shard_map/all_gather | solution.py:111
  258.0 130.5 %all-gather.7.cloned.1.call-start = ((), (), s32[]{:S(2)}) async-start(), calls=%async_computation.9 | async-start | bytes 2949120 | tf_op jit(solution)/shard_map/all_gather | solution.py:111
  311.8 17.9 %copy-start.16 = (bf16[192,4,48,1,1]{0,2,1,4,3:T(8,128)(2,1)S(1)}, bf16[192,4,48,1,1]{0,2,1,4,3:T(8,128)(2,1)}, u32[]{:S(2)}) copy-start(bf16[192,4,48,1,1]{0,2,1,4,3:T(8,128)(2,1)} %constant.113) | copy-start | bytes 221188
  330.6 1.3 copy-start.3
  330.6 1.6 copy-start.5
  330.6 1.6 copy-start.13
  332.2 6.2 %copy-start.6 = (f32[2,24,48,192]{3,2,1,0:T(8,128)}, f32[2,24,48,192]{3,2,1,0:T(8,128)S(1)}, u32[]{:S(2)}) copy-start(f32[2,24,48,192]{3,2,1,0:T(8,128)S(1)} %fusion.20) | copy-start | bytes 5308420
  338.5 100.4 %all-gather.11.cloned.1.call-start = ((), (), s32[]{:S(2)}) async-start(), calls=%async_computation.11 | async-start | bytes 2949120 | tf_op jit(solution)/shard_map/all_gather | solution.py:111
  340.7 148.4 %all-gather.5.cloned.1.call-start = ((), (), s32[]{:S(2)}) async-start(), calls=%async_computation.8 | async-start | bytes 2949120 | tf_op jit(solution)/shard_map/all_gather | solution.py:111
  438.9 54.7 %copy-start.1 = (bf16[1,128,384]{2,1,0:T(8,128)(2,1)S(1)}, bf16[1,128,384]{2,1,0:T(8,128)(2,1)}, u32[]{:S(2)}) copy-start(bf16[1,128,384]{2,1,0:T(8,128)(2,1)} %param.24) | copy-start | bytes 294916
  (3 other events, 2.7 us)
Sparse Core Ops, SparseCore 0:
  259.6 58.5 all-gather.8
  338.6 49.8 all-gather.6
  390.1 48.7 all-gather.10
  440.3 48.7 all-gather.4

commit v2 on v1

--- a/solution.py
+++ b/solution.py
@@ -136,12 +136,13 @@
     derive = derivative_matrix(points).astype(np.float32)
     basis32 = basis.astype(np.float32)
     data = jnp.einsum("yzx,xpk->pyzk", rho, basis32.reshape(points, rows_px, xblock), precision=HIGH)
+    grad_x = jnp.einsum("yzx,xw->zyw", rho, derive, precision=HIGH)
+    data, grad_x_sent = lax.optimization_barrier((data, grad_x.astype(BF)))
+    every_x = gathered(grad_x_sent)
     data = lax.all_to_all(data, "px", split_axis=0, concat_axis=0, tiled=True)
     data = data.reshape(points, zshare, xblock)
     high_basis, low_basis = two_halves(basis)
     x_basis = (high_basis.reshape(points, rows_px, xblock), low_basis.reshape(points, rows_px, xblock))
-    grad_x = jnp.einsum("yzx,xw->zyw", rho, derive, precision=HIGH)
-    every_x = gathered(grad_x)
     lines_y = jnp.einsum("yzk,yw->wzk", data, derive, precision=HIGH).astype(BF)
     lines_y = lines_y.reshape(rows_px, yblock, zshare, xblock)
     lines_y = lax.all_to_all(lines_y, "px", split_axis=0, concat_axis=0, tiled=True)
@@ -170,7 +171,7 @@
         ],
         1,
     )
-    back, every_y = lax.optimization_barrier((back, grad_y_sent))
+    back, every_y, every_x = lax.optimization_barrier((back, grad_y_sent, every_x))
     every_y = gathered(every_y)
     back = lax.all_to_all(back, ("band", "py"), split_axis=0, concat_axis=0, tiled=True)
     y_basis = (high_basis.reshape(points, pieces, kyblock), low_basis.reshape(points, pieces, kyblock))

time: 508 us -> 499 us (0.982)
  waiting for transfers between devices: 303 us -> 273 us
  local copies, waits for them, and re-layouts: 50.4 us -> 61.4 us
  other arithmetic: 28.8 us -> 33.9 us
    all_gather x4, waiting for transfers between devices: 137 us -> 84.3 us  [gathered(): return lax.all_gather(field, 'band', axis=0, tiled=True)]
    all_to_all x1, waiting for transfers between devices: 17.7 us -> 41.6 us  [body(): lax.all_to_all(modes, ('band', 'py'), split_axis=0, concat_axis=0, tiled=...]
    unnamed x64 -> x56, local copies, waits for them, and re-layouts: 31.8 us -> 41.8 us
    convert_element_type x0 -> x2, other arithmetic: none -> 6.17 us  [the longest x1 5.2 us: gathered(): field = with_layout_constraint(field.astype(BF), Layout((0, 1, 2)))]
  transfers between devices with their start and end apart: 10 -> 10, of which waited for: 9 -> 7; matrix products, arithmetic and copies ran while one was open for 10% -> 14% of each run, Pallas kernels for 0% -> 0%
where the time goes in v2:
time: 499 us; the launch traced here: 491 us
  waiting for transfers between devices  273 us (55%)
  local copies, waits for them, and re-layouts  61.4 us (12%)
  matrix products  47 us (9%)
  other arithmetic  33.9 us (7%)
  blocking collectives  32 us (6%)
  starting transfers between devices  27.7 us (6%)
  between operations  15.2 us (3%)
    all_gather x4, waiting for transfers between devices, gathered(): return lax.all_gather(field, 'band', axis=0, tiled=True)  84.3 us
    all_to_all x1, waiting for transfers between devices, body(): lax.all_to_all(shares, 'band', split_axis=0, concat_axis=0, tiled=True)  53.5 us
    all_to_all x1, waiting for transfers between devices, partial_density(): plane = lax.all_to_all(plane, 'px', split_axis=0, concat_axis=0, tiled=True)  53.2 us
    unnamed x56, local copies, waits for them, and re-layouts  41.8 us
    all_to_all x1, waiting for transfers between devices, body(): lax.all_to_all(modes, ('band', 'py'), split_axis=0, concat_axis=0, tiled=...  41.6 us
    all_to_all x1, waiting for transfers between devices, body(): lax.all_to_all(back, ('band', 'py'), split_axis=0, concat_axis=0, tiled=T...  36.3 us
    all_to_all x1, blocking collectives, body(): data = lax.all_to_all(data, 'px', split_axis=0, concat_axis=0, tiled=True)  16.1 us
    all_to_all x1, blocking collectives, body(): lines = lax.all_to_all(lines, 'px', split_axis=1, concat_axis=1, tiled=True)  15.8 us
  transfers between devices with their start and end apart: 10, of which 7 were waited for; matrix products, arithmetic and copies ran while one was open for 14% of the time, Pallas kernels for 0%

profile of v2, /device:TPU:0, one launch (start us, length us, event | category | flops | bytes accessed | tf_op | source)
XLA Modules:
  0.0 490.6 jit_solution(10835476678596316135)
XLA Ops:
  13.1 4.3 all-to-all-start
  18.1 3.6 all-to-all-done
  22.0 5.3 %fusion.4 = f32[4,48,2,48,96,1]{4,1,5,3,2,0:T(8,128)} fusion(pred[256,48]{0,1:T(8,128)(4,1)S(1)} %iota_compare_fusion.1, bf16[256,2,96]{0,2,1:T(8,128)(2,1)S(1)} %broadcast_in_dim.35, bf16[192,2,4,48,2]{0,3,1,4,2:T(8,128)(2,1)S(1)} %copy-done.20, s32[256]{0:T(256)S(1)} %bitcast.243), kind=kOutput, calls=%fused_computation.9 | convolution fusion | flops 1890041856 | bytes 7484416 | tf_op jit(solution)/shard_map/sipwo,sixz->pwoxz/dot_general | solution.py:100
  27.4 6.9 %fusion = bf16[4,48,2,48,96]{4,1,3,2,0:T(8,128)(2,1)} fusion(f32[4,48,2,48,96,1]{4,1,5,3,2,0:T(8,128)} %fusion.4, pred[256,48]{0,1:T(8,128)(4,1)S(1)} %iota_compare_fusion.1, bf16[256,2,96]{0,2,1:T(8,128)(2,1)S(1)} %broadcast_in_dim.35, bf16[192,2,4,48,2]{0,3,1,4,2:T(8,128)(2,1)S(1)} %copy-done.19, s32[256]{0:T(256)S(1)} %bitcast.244), kind=kOutput, calls=%fused_computation.2 | convolution fusion | flops 1893580800 | bytes 11023360 | tf_op jit(solution)/shard_map/sipwo,sixz->pwoxz/dot_general | solution.py:99
  34.3 5.1 %all-to-all-start.1 = ((bf16[4,48,2,48,96]{4,1,3,2,0:T(8,128)(2,1)}), bf16[4,48,2,48,96]{4,1,3,2,0:T(8,128)(2,1)}, u32[]{:S(2)}, u32[]{:S(2)}) async-start(bf16[4,48,2,48,96]{4,1,3,2,0:T(8,128)(2,1)} %fusion), calls=%async_computation.1 | async-start | bytes 9437184 | tf_op jit(solution)/shard_map/all_to_all | solution.py:102
  40.0 53.2 %all-to-all-done.1 = bf16[4,48,2,48,96]{4,1,3,2,0:T(8,128)(2,1)} async-done(((bf16[4,48,2,48,96]{4,1,3,2,0:T(8,128)(2,1)}), bf16[4,48,2,48,96]{4,1,3,2,0:T(8,128)(2,1)}, u32[]{:S(2)}, u32[]{:S(2)}) %all-to-all-start.1) | async-done | bytes 3538976 | tf_op jit(solution)/shard_map/all_to_all | solution.py:102
  93.2 5.6 %fusion.12 = f32[48,96,2,192,1,1]{3,1,5,4,2,0:T(8,128)S(1)} fusion(bf16[4,2,48,2,192,1]{4,2,0,1,3,5:T(8,128)(2,1)S(1)} %copy-done.10, bf16[4,48,2,48,96,1]{4,1,3,2,0,5:T(8,128)(2,1)} %bitcast.21), kind=kOutput, calls=%fused_computation.18 | convolution fusion | flops 1358954496 | bytes 10911744 | tf_op jit(solution)/shard_map/pwoxz,poxtk->wztk/dot_general | solution.py:36
  98.8 5.6 %bitcast_add_fusion = f32[48,96,2,192]{3,1,2,0:T(8,128)S(1)} fusion(f32[48,96,2,192,1,1]{3,1,5,4,2,0:T(8,128)S(1)} %fusion.12, bf16[4,2,48,2,192,1]{4,2,0,1,3,5:T(8,128)(2,1)S(1)} %copy-done.9, bf16[4,48,2,48,96,1]{4,1,3,2,0,5:T(8,128)(2,1)} %bitcast.21), kind=kOutput, calls=%fused_computation | convolution fusion | flops 1360723968 | bytes 17989632 | tf_op jit(solution)/shard_map/pwoxz,poxtk->wztk/dot_general | solution.py:35
  107.2 5.5 %all-to-all-start.2 = ((bf16[4,48,24,192]{3,2,1,0:T(8,128)(2,1)}), bf16[4,48,24,192]{3,2,1,0:T(8,128)(2,1)S(1)}, u32[]{:S(2)}, u32[]{:S(2)}) async-start(bf16[4,48,24,192]{3,2,1,0:T(8,128)(2,1)} %bitcast.229), calls=%async_computation.2 | async-start | bytes 4718592 | tf_op jit(solution)/shard_map/all_to_all | solution.py:131
  112.7 53.5 %all-to-all-done.2 = bf16[4,48,24,192]{3,2,1,0:T(8,128)(2,1)S(1)} async-done(((bf16[4,48,24,192]{3,2,1,0:T(8,128)(2,1)}), bf16[4,48,24,192]{3,2,1,0:T(8,128)(2,1)S(1)}, u32[]{:S(2)}, u32[]{:S(2)}) %all-to-all-start.2) | async-done | bytes 1769504 | tf_op jit(solution)/shard_map/all_to_all | solution.py:131
  174.5 3.1 reshape.140
  177.6 16.1 %all_to_all.50 = f32[4,1,55296]{2,1,0:T(1,128)S(1)} all-to-all(f32[4,1,55296]{2,1,0:T(1,128)} %reshape.140), channel_id=1, replica_groups=mesh['band'=4,'px'=4,'py'=2] {'px'}, dimensions={0} | all-to-all | bytes 1769472 | tf_op jit(solution)/shard_map/all_to_all | solution.py:142
  194.3 3.2 reduce.1
  208.5 4.1 all-to-all-start.5
  218.2 3.2 reshape.142
  221.4 3.7 all-to-all-start.4
  230.6 41.6 %all-to-all-done.4 = f32[8,1,27648]{2,1,0:T(1,128)S(1)} async-done(((f32[8,1,27648]{2,1,0:T(1,128)}), f32[8,1,27648]{2,1,0:T(1,128)S(1)}, u32[]{:S(2)}, u32[]{:S(2)}) %all-to-all-start.4) | async-done | bytes 884768 | tf_op jit(solution)/shard_map/all_to_all | solution.py:153
  277.3 4.1 fusion.50
  287.0 6.6 %reshape.146 = bf16[8,2,27648]{2,1,0:T(2,128)(2,1)} reshape(bf16[8,2,24,24,48]{4,3,2,1,0:T(8,128)(2,1)} %copy.110) | data formatting | bytes 1769472
  293.6 4.2 all-to-all-start.6
  298.6 36.3 %all-to-all-done.6 = bf16[8,2,27648]{2,1,0:T(2,128)(2,1)} async-done(((bf16[8,2,27648]{2,1,0:T(2,128)(2,1)}), bf16[8,2,27648]{2,1,0:T(2,128)(2,1)}, u32[]{:S(2)}, u32[]{:S(2)}) %all-to-all-start.6) | async-done | bytes 884768 | tf_op jit(solution)/shard_map/all_to_all | solution.py:176
  334.9 3.8 reshape.147
  342.3 4.0 reshape.102
  346.3 3.5 copy.113
  349.8 4.8 reshape.148
  354.6 15.8 %all_to_all.51 = bf16[4,2,55296]{2,1,0:T(2,128)(2,1)} all-to-all(bf16[4,2,55296]{2,1,0:T(2,128)(2,1)S(1)} %reshape.148), channel_id=1, replica_groups=mesh['band'=4,'px'=4,'py'=2] {'px'}, dimensions={0} | all-to-all | bytes 1769472 | tf_op jit(solution)/shard_map/all_to_all | solution.py:180
  370.4 3.6 reshape.149
  379.3 5.2 %fusion.58 = bf16[24,48,192]{2,1,0:T(8,128)(2,1)} fusion(f32[2,24,48,192]{3,2,1,0:T(8,128)} %copy-done.2, f32[48,24,192]{2,0,1:T(8,128)S(1)} %copy-done.4, f32[48,24,192]{2,0,1:T(8,128)} %copy-done.5, f32[48,24,192]{2,1,0:T(8,128)S(1)} %convert_reduce_fusion, f32[96,48,192]{2,1,0:T(8,128)} %param.27, s32[]{:T(128)S(6)} %select_n.21), kind=kLoop, calls=%fused_computation.68 | loop fusion | flops 5308416 | bytes 5750788 | tf_op jit(solution)/shard_map/convert_element_type | solution.py:110
  384.5 44.6 %all-gather.11.cloned.1.call-done = bf16[96,48,192]{2,1,0:T(8,128)(2,1)} async-done(((bf16[24,48,192]{2,1,0:T(8,128)(2,1)}), bf16[96,48,192]{2,1,0:T(8,128)(2,1)}) %all-gather.11.cloned.1.call-update) | async-done | bytes 1769488 | tf_op jit(solution)/shard_map/all_gather | solution.py:111
  429.1 10.5 %maximum_convert_fusion = f32[3,96,48,192]{3,2,1,0:T(8,128)} fusion(bf16[1,96,48,192]{3,2,1,0:T(8,128)(2,1)} %bitcast.238, bf16[1,96,48,192]{3,2,1,0:T(8,128)(2,1)} %bitcast.237, bf16[1,96,48,192]{3,2,1,0:T(8,128)(2,1)} %bitcast.236), kind=kLoop, calls=%fused_computation.3 | loop fusion | flops 7962624 | bytes 15925248 | tf_op jit(solution)/shard_map/stack | solution.py:185
  439.6 39.7 %all-gather.7.cloned.1.call-done = bf16[96,48,192]{2,1,0:T(8,128)(2,1)} async-done(((bf16[24,48,192]{2,1,0:T(8,128)(2,1)}), bf16[96,48,192]{2,1,0:T(8,128)(2,1)}) %all-gather.7.cloned.1.call-update) | async-done | bytes 1769488 | tf_op jit(solution)/shard_map/all_gather | solution.py:111
  479.3 4.5 convert_element_type.98
  (99 shorter events, 60.7 us)
Async XLA Ops:
  7.2 0.9 copy-start
  7.2 14.8 %copy-start.20 = (bf16[192,2,4,48,2]{0,3,1,4,2:T(8,128)(2,1)S(1)}, bf16[192,2,4,48,2]{0,3,1,4,2:T(8,128)(2,1)}, u32[]{:S(2)}) copy-start(bf16[192,2,4,48,2]{0,3,1,4,2:T(8,128)(2,1)} %constant.87.clone) | copy-start | bytes 884740
  13.1 8.6 %all-to-all-start = ((bf16[2,2,12288]{2,1,0:T(2,128)(2,1)}), bf16[2,2,12288]{2,1,0:T(2,128)(2,1)S(1)}, u32[]{:S(2)}, u32[]{:S(2)}) async-start(bf16[2,2,12288]{2,1,0:T(2,128)(2,1)} %reshape.138), calls=%async_computation | async-start | bytes 196608 | tf_op jit(solution)/shard_map/all_to_all | solution.py:84
  22.0 5.4 %copy-start.19 = (bf16[192,2,4,48,2]{0,3,1,4,2:T(8,128)(2,1)S(1)}, bf16[192,2,4,48,2]{0,3,1,4,2:T(8,128)(2,1)}, u32[]{:S(2)}) copy-start(bf16[192,2,4,48,2]{0,3,1,4,2:T(8,128)(2,1)} %constant.86.clone) | copy-start | bytes 884740
  34.3 58.9 %copy-start.10 = (bf16[4,2,48,2,192,1]{4,2,0,1,3,5:T(8,128)(2,1)S(1)}, bf16[4,2,48,2,192,1]{4,2,0,1,3,5:T(8,128)(2,1)}, u32[]{:S(2)}) copy-start(bf16[4,2,48,2,192,1]{4,2,0,1,3,5:T(8,128)(2,1)} %constant.104) | copy-start | bytes 884740
  34.3 58.9 %all-to-all-start.1 = ((bf16[4,48,2,48,96]{4,1,3,2,0:T(8,128)(2,1)}), bf16[4,48,2,48,96]{4,1,3,2,0:T(8,128)(2,1)}, u32[]{:S(2)}, u32[]{:S(2)}) async-start(bf16[4,48,2,48,96]{4,1,3,2,0:T(8,128)(2,1)} %fusion), calls=%async_computation.1 | async-start | bytes 9437184 | tf_op jit(solution)/shard_map/all_to_all | solution.py:102
  93.2 5.6 %copy-start.9 = (bf16[4,2,48,2,192,1]{4,2,0,1,3,5:T(8,128)(2,1)S(1)}, bf16[4,2,48,2,192,1]{4,2,0,1,3,5:T(8,128)(2,1)}, u32[]{:S(2)}) copy-start(bf16[4,2,48,2,192,1]{4,2,0,1,3,5:T(8,128)(2,1)} %constant.103) | copy-start | bytes 884740
  107.2 59.1 %all-to-all-start.2 = ((bf16[4,48,24,192]{3,2,1,0:T(8,128)(2,1)}), bf16[4,48,24,192]{3,2,1,0:T(8,128)(2,1)S(1)}, u32[]{:S(2)}, u32[]{:S(2)}) async-start(bf16[4,48,24,192]{3,2,1,0:T(8,128)(2,1)} %bitcast.229), calls=%async_computation.2 | async-start | bytes 4718592 | tf_op jit(solution)/shard_map/all_to_all | solution.py:131
  166.6 1.8 copy-start.7
  168.4 4.4 copy-start.11
  170.7 1.1 copy-start.5
  200.0 2.4 copy-start.8
  208.5 12.9 %all-to-all-start.5 = ((bf16[4,2,27648]{2,1,0:T(2,128)(2,1)}), bf16[4,2,27648]{2,1,0:T(2,128)(2,1)}, u32[]{:S(2)}, u32[]{:S(2)}) async-start(bf16[4,2,27648]{2,1,0:T(2,128)(2,1)} %reshape.144), calls=%async_computation.5 | async-start | bytes 884736 | tf_op jit(solution)/shard_map/all_to_all | solution.py:148
  212.6 72.4 %all-gather.5.cloned.1.call-start = ((), (), s32[]{:S(2)}) async-start(), calls=%async_computation.8 | async-start | bytes 2949120 | tf_op jit(solution)/shard_map/all_gather | solution.py:111
  218.2 7.0 %copy-start.17 = (f32[192]{0:T(256)S(1)}, f32[192]{0:T(256)}, u32[]{:S(2)}) copy-start(f32[192]{0:T(256)} %constant.96.clone) | copy-start | bytes 2308
  221.4 6.4 %copy-start.14 = (bf16[192,4,48,1]{0,2,1,3:T(8,128)(2,1)S(1)}, bf16[192,4,48,1]{0,2,1,3:T(8,128)(2,1)}, u32[]{:S(2)}) copy-start(bf16[192,4,48,1]{0,2,1,3:T(8,128)(2,1)} %constant.109) | copy-start | bytes 221188
  221.4 50.8 %all-to-all-start.4 = ((f32[8,1,27648]{2,1,0:T(1,128)}), f32[8,1,27648]{2,1,0:T(1,128)S(1)}, u32[]{:S(2)}, u32[]{:S(2)}) async-start(f32[8,1,27648]{2,1,0:T(1,128)} %reshape.142), calls=%async_computation.4 | async-start | bytes 1769472 | tf_op jit(solution)/shard_map/all_to_all | solution.py:153
  225.1 3.2 copy-start.16
  228.7 1.0 copy-start.3
  230.6 46.8 %copy-start.12 = (f32[8,24,192,1]{2,1,0,3:T(8,128)S(1)}, f32[8,24,192,1]{2,1,0,3:T(8,128)}, u32[]{:S(2)}) copy-start(f32[8,24,192,1]{2,1,0,3:T(8,128)} %constant.102) | copy-start | bytes 442372
  277.3 5.2 %copy-start.18 = (f32[8,24,8,24,1]{1,3,0,2,4:T(8,128)S(1)}, f32[8,24,8,24,1]{1,3,0,2,4:T(8,128)}, u32[]{:S(2)}) copy-start(f32[8,24,8,24,1]{1,3,0,2,4:T(8,128)} %constant.107) | copy-start | bytes 442372
  281.4 1.7 copy-start.6
  293.6 41.3 %all-to-all-start.6 = ((bf16[8,2,27648]{2,1,0:T(2,128)(2,1)}), bf16[8,2,27648]{2,1,0:T(2,128)(2,1)}, u32[]{:S(2)}, u32[]{:S(2)}) async-start(bf16[8,2,27648]{2,1,0:T(2,128)(2,1)} %reshape.146), calls=%async_computation.6 | async-start | bytes 1769472 | tf_op jit(solution)/shard_map/all_to_all | solution.py:176
  297.8 86.7 %all-gather.9.cloned.1.call-start = ((), (), s32[]{:S(2)}) async-start(), calls=%async_computation.10 | async-start | bytes 2949120 | tf_op jit(solution)/shard_map/all_gather | solution.py:111
  298.6 130.5 %all-gather.11.cloned.1.call-start = ((), (), s32[]{:S(2)}) async-start(), calls=%async_computation.11 | async-start | bytes 2949120 | tf_op jit(solution)/shard_map/all_gather | solution.py:111
  338.8 1.7 copy-start.15
  374.0 1.6 copy-start.13
  376.4 1.4 copy-start.2
  377.8 1.5 copy-start.4
  378.7 100.6 %all-gather.7.cloned.1.call-start = ((), (), s32[]{:S(2)}) async-start(), calls=%async_computation.9 | async-start | bytes 2949120 | tf_op jit(solution)/shard_map/all_gather | solution.py:111
  429.1 54.7 %copy-start.1 = (bf16[1,128,384]{2,1,0:T(8,128)(2,1)S(1)}, bf16[1,128,384]{2,1,0:T(8,128)(2,1)}, u32[]{:S(2)}) copy-start(bf16[1,128,384]{2,1,0:T(8,128)(2,1)} %param.24) | copy-start | bytes 294916
Sparse Core Ops, SparseCore 0:
  215.0 67.5 all-gather.4
  300.2 58.6 all-gather.8
  378.8 50.2 all-gather.10
  430.5 48.7 all-gather.6
